TPU v7x, 32 devices: a whole 2x2x4 slice. The times are simulated.
32 devices in a mesh: grid: 8 (over y, x, core), atom: 4 (over z).
Axes of the slice: x: 2, y: 2, z: 4, core: 2. Of those that a mesh axis runs over, the one named last changes fastest.
Arguments:
- basis_values: bfloat16 [64, 128, 512], P(('grid', 'atom')), may hold values from -8 to 8
- block_lists: int32 [64, 4], P('grid'), may hold values from 0 to 95, as said below
- orbitals: bfloat16 [12288, 4096], P('grid', 'atom'), may hold values from -0.00390625 to 0.00390625
- point_weights: float32 [8192], P(('grid', 'atom')), may hold values from 0.1 to 1
- point_atoms: int32 [8192], P(('grid', 'atom')), may hold values from 0 to 127, as said below
- embed_scale: float32 [256], replicated, may hold values from -4 to 4
- embed_shift: float32 [256], replicated, may hold values from -3 to 3
- message_weight: bfloat16 [2, 256, 256], replicated, may hold values from -0.375 to 0.375
- atom_weight: bfloat16 [2, 256, 256], replicated, may hold values from -0.375 to 0.375
- head_weight: float32 [256], replicated, may hold values from -0.375 to 0.375
Outputs:
- fock_orbitals: float32 [12288, 4096], P('grid', 'atom')
- potential: float32 [8192], P(('grid', 'atom'))
Inputs may be any that keep to these rules, and one draw needn't show every extreme that they name: `block_lists`: each row names 4 different blocks; a batch b of group g = b // 8 names only blocks (g - 1) * 12 to (g + 2) * 12 - 1. `point_atoms`: the 256 points of one device name atom centres of one run of max(8, 1) consecutive centres, counted round.
All inputs are finite; a program needn't handle non-finite values.
Results may differ from a plain program's by a relative error of at most 0.04.
Values may be sent and summed in bfloat16 or wider, within the bound.
A program may use at most 128 MiB of HBM per device.

v0:
```python
import jax
import jax.numpy as jnp
from jax import lax
from jax.sharding import PartitionSpec as P

ATOM_DEV = 32


def padded(cells, sides, width):
    for axis, dim in sides:
        count = lax.axis_size(axis)
        ends = count - 1
        head = lax.slice_in_dim(cells, 0, width, axis=dim)
        tail = lax.slice_in_dim(cells, cells.shape[dim] - width, cells.shape[dim], axis=dim)
        cells = jnp.concatenate(
            [
                lax.ppermute(tail, axis, [(i, (i + 1) % count) for i in range(ends)]),
                cells,
                lax.ppermute(head, axis, [((i + 1) % count, i) for i in range(ends)]),
            ],
            axis=dim,
        )
    return cells


def passed_along(value, axis, steps):
    count = lax.axis_size(axis)
    leading, last = (max(0, -steps), min(count, count - steps))
    return lax.ppermute(value, axis, [(source, source + steps) for source in range(leading, last)])


def orbital_values(piece, lists, blocks):
    count = piece.shape[0]
    chosen = blocks[lists].reshape(count, -1, blocks.shape[2])
    values = jnp.einsum("bpk,bko->bpo", piece, chosen, preferred_element_type=jnp.float32)
    return values.astype(jnp.bfloat16)


def fock_terms(piece, lists, psi_rows, scale_rows, total):
    weighted_psi = (scale_rows[:, :, None] * psi_rows.astype(jnp.float32)).astype(jnp.bfloat16)
    terms = jnp.einsum("bpk,bpo->bko", piece, weighted_psi, preferred_element_type=jnp.float32)
    terms = terms.reshape(-1, total.shape[1], total.shape[2])
    return total.at[lists.reshape(-1)].add(terms)


def atom_update(rows, mass, weight):
    mean = rows / (1.0 + mass[:, None])
    return jax.nn.silu(
        jnp.dot(mean.astype(jnp.bfloat16), weight, preferred_element_type=jnp.float32)
    ).astype(jnp.bfloat16)


def local(
    basis_values,
    block_lists,
    orbitals,
    point_weights,
    point_atoms,
    embed_scale,
    embed_shift,
    message_weight,
    atom_weight,
    head_weight,
):
    own_rows = orbitals.shape[0]
    gathered = padded(orbitals, (("grid", 0),), own_rows)
    width = basis_values.shape[2] // block_lists.shape[1]
    owned = own_rows // width
    blocks = gathered.reshape(-1, width, gathered.shape[1])
    offset = (lax.axis_index("grid") - 1) * owned
    local_lists = block_lists - offset
    group_values = lax.all_gather(basis_values, "atom", axis=0, tiled=True)
    psi = orbital_values(group_values, local_lists, blocks)
    squares = 2.0 * jnp.sum(jnp.square(psi.astype(jnp.float32)), axis=2).reshape(-1)
    density = lax.psum_scatter(squares, "atom", scatter_dimension=0, tiled=True)
    radius = jnp.cbrt(density)
    hidden = jax.nn.silu(radius[:, None] * embed_scale[None, :] + embed_shift[None, :])
    atom_total = ATOM_DEV * lax.axis_size("atom")
    onehot = point_atoms[:, None] == jnp.arange(atom_total, dtype=jnp.int32)[None, :]
    selector = onehot.astype(jnp.bfloat16)
    counts = jnp.dot(point_weights, onehot.astype(jnp.float32), precision=lax.Precision.HIGHEST)
    for layer in range(message_weight.shape[0]):
        message = jax.nn.silu(
            jnp.dot(
                hidden.astype(jnp.bfloat16),
                message_weight[layer],
                preferred_element_type=jnp.float32,
            )
        )
        weighted = (point_weights[:, None] * message).astype(jnp.bfloat16)
        partial_value = lax.dot_general(
            selector, weighted, (((0,), (0,)), ((), ())), preferred_element_type=jnp.float32
        )
        rows, mass = (
            lax.psum_scatter(
                partial_value.astype(jnp.bfloat16), "atom", scatter_dimension=0, tiled=True
            ).astype(jnp.float32),
            lax.psum_scatter(
                counts.astype(jnp.bfloat16), "atom", scatter_dimension=0, tiled=True
            ).astype(jnp.float32),
        )
        rows, mass = (
            lax.psum(rows.astype(jnp.bfloat16), "grid").astype(jnp.float32),
            lax.psum(mass.astype(jnp.bfloat16), "grid").astype(jnp.float32),
        )
        update = atom_update(rows, mass, atom_weight[layer])
        features = lax.all_gather(update, "atom", axis=0, tiled=True)
        picked = jnp.dot(selector, features, preferred_element_type=jnp.float32)
        hidden = hidden + message * picked
    score = jnp.dot(hidden, head_weight, precision=lax.Precision.HIGHEST)
    potential = radius * (1.0 + jnp.tanh(score))
    scaled = lax.all_gather(point_weights * potential, "atom", axis=0, tiled=True)
    scaled = scaled.reshape(psi.shape[0], psi.shape[1])
    empty = jnp.zeros((blocks.shape[0], width, psi.shape[2]), jnp.float32)
    total = fock_terms(group_values, local_lists, psi, scaled, empty)
    rounded = lax.optimization_barrier(
        total.reshape(3, own_rows, total.shape[2]).astype(jnp.bfloat16)
    )
    from_below = passed_along(rounded[2], "grid", 1)
    from_above = passed_along(rounded[0], "grid", -1)
    fock_orbitals = (
        rounded[1].astype(jnp.float32)
        + from_below.astype(jnp.float32)
        + from_above.astype(jnp.float32)
    )
    return (fock_orbitals, potential)


def solution(mesh):
    return jax.shard_map(
        local,
        mesh=mesh,
        in_specs=(
            P(("grid", "atom"), None, None),
            P("grid", None),
            P("grid", "atom"),
            P(("grid", "atom")),
            P(("grid", "atom")),
            P(),
            P(),
            P(),
            P(),
            P(),
        ),
        out_specs=(P("grid", "atom"), P(("grid", "atom"))),
        check_vma=False,
    )
```

profile of v0, /device:TPU:1, one launch (start us, length us, event | category | flops | bytes accessed | tf_op | source)
XLA Modules:
  0.0 383.1 jit_solution(17801122140071858288)
XLA Ops:
  7.2 4.5 %collective-permute-start = (bf16[1536,1024]{1,0:T(8,128)(2,1)}, bf16[1536,1024]{1,0:T(8,128)(2,1)S(1)}, u32[]{:S(2)}, u32[]{:S(2)}) collective-permute-start(bf16[1536,1024]{1,0:T(8,128)(2,1)} %param.12), channel_id=1, source_target_pairs={{0,4},{4,8},{8,12},{12,16},{16,20},{20,24},{24,28},{1,5},{5,9},{9,... | collective-permute-start | bytes 9437192 | tf_op jit(solution)/shard_map/ppermute | solution.py:17
  11.7 1.9 collective-permute-start.1
  13.7 0.0 reduce-scatter.3.cloned.1.call-start
  13.7 1.2 dynamic-slice
  16.3 0.7 compare_select_fusion
  17.0 0.1 copy.20
  17.1 0.1 reshape.66
  17.1 0.1 copy.19
  17.2 0.1 reshape.59
  17.3 28.9 %collective-permute-done = bf16[1536,1024]{1,0:T(8,128)(2,1)S(1)} collective-permute-done((bf16[1536,1024]{1,0:T(8,128)(2,1)}, bf16[1536,1024]{1,0:T(8,128)(2,1)S(1)}, u32[]{:S(2)}, u32[]{:S(2)}) %collective-permute-start) | collective-permute-done | bytes 3145760 | tf_op jit(solution)/shard_map/ppermute | solution.py:17
  46.2 35.4 %collective-permute-done.1 = bf16[1536,1024]{1,0:T(8,128)(2,1)} collective-permute-done((bf16[1536,1024]{1,0:T(8,128)(2,1)}, bf16[1536,1024]{1,0:T(8,128)(2,1)}, u32[]{:S(2)}, u32[]{:S(2)}) %collective-permute-start.1) | collective-permute-done | bytes 3145760 | tf_op jit(solution)/shard_map/ppermute | solution.py:19
  81.6 7.0 %pad_maximum_fusion = bf16[4608,1024]{1,0:T(8,128)(2,1)} fusion(bf16[1536,1024]{1,0:T(8,128)(2,1)} %collective-permute-done.1, bf16[1536,1024]{1,0:T(8,128)(2,1)} %param.12, bf16[1536,1024]{1,0:T(8,128)(2,1)S(1)} %collective-permute-done), kind=kLoop, calls=%fused_computation.2 | loop fusion | flops 28311552 | bytes 18874368 | tf_op jit(solution)/shard_map/concatenate | solution.py:15
  88.6 8.8 %gather_fusion = bf16[32,128,1024]{2,1,0:T(8,128)(2,1)} fusion(bf16[36,128,1024]{2,1,0:T(8,128)(2,1)} %bitcast.59, s32[1024]{0:T(1024)S(1)} %pad_clamp_fusion), kind=kCustom, calls=%fused_computation | custom fusion | bytes 16777344 | tf_op jit(solution)/shard_map/gather | solution.py:34
  97.4 6.4 %fusion.1 = (f32[8,128]{1,0:T(8,128)S(1)}, bf16[8,1024,128]{2,1,0:T(8,128)(2,1)S(1)}) fusion(bf16[8,512,1024]{2,1,0:T(8,128)(2,1)} %bitcast.60, bf16[8,128,512]{2,1,0:T(8,128)(2,1)} %all-gather.3.cloned.1.call-done), kind=kOutput, calls=%fused_computation.7 | convolution fusion | flops 1077935104 | bytes 11538432 | tf_op jit(solution)/shard_map/bpk,bko->bpo/dot_general | solution.py:35
  103.8 10.1 %all-reduce = f32[1024]{0:T(1024)S(1)} all-reduce(f32[1024]{0:T(1024)S(1)} %multiply_bitcast_fusion), channel_id=2, replica_groups=mesh['grid'=8,'atom'=4] {'atom'}, use_global_device_ids=true, to_apply=%region_1.0.clone | all-reduce | flops 1024 | bytes 8192
  113.9 0.1 dynamic-slice_cbrt_fusion
  114.0 1.2 divide_multiply_fusion.1
  115.2 0.9 convolution_convert_fusion.2
  116.2 0.0 reduce-scatter.5.cloned.1.call-start
  116.3 0.2 fusion.8
  116.5 6.7 %all-reduce.1 = bf16[128]{0:T(256)(128)(2,1)S(1)} all-reduce(bf16[128]{0:T(256)(128)(2,1)S(1)} %fusion.8), channel_id=4, replica_groups=mesh['grid'=8,'atom'=4] {'atom'}, use_global_device_ids=true, to_apply=%region_4.5.clone | all-reduce | flops 128 | bytes 512
  123.1 0.1 dynamic-slice.3
  123.2 7.5 %reduce-scatter.3.cloned.1.call-done = bf16[32,256]{1,0:T(8,128)(2,1)} async-done(((bf16[128,256]{1,0:T(8,128)(2,1)}), bf16[32,256]{1,0:T(8,128)(2,1)}) %reduce-scatter.3.cloned.1.call-update) | async-done | bytes 16400 | tf_op jit(solution)/shard_map/reduce_scatter | solution.py:95
  130.7 22.6 %all-reduce.2 = (bf16[32,256]{1,0:T(8,128)(2,1)S(1)}, bf16[32]{0:T(256)(128)(2,1)S(1)}) all-reduce(bf16[32,256]{1,0:T(8,128)(2,1)} %reduce-scatter.3.cloned.1.call-done, bf16[32]{0:T(256)(128)(2,1)S(1)} %dynamic-slice.3), channel_id=1, replica_groups=mesh['grid'=8,'atom'=4] {'grid'}, use_global_device_ids=true, to_apply=%region_3.4 | all-reduce | flops 8224 | bytes 32896 | tf_op jit(solution)/shard_map/psum | solution.py:103
  153.4 1.1 multiply_convert_fusion.5
  154.5 10.3 %all_gather.13 = bf16[128,256]{1,0:T(8,128)(2,1)S(1)} all-gather(bf16[32,256]{1,0:T(8,128)(2,1)S(1)} %multiply_convert_fusion.5), channel_id=1, replica_groups=mesh['grid'=8,'atom'=4] {'atom'}, dimensions={0}, use_global_device_ids=true | all-gather | bytes 81920 | tf_op jit(solution)/shard_map/all_gather | solution.py:107
  164.8 0.2 fusion.7
  165.1 0.7 copy-done.3
  165.8 1.1 divide_multiply_fusion
  166.9 0.9 convolution_convert_fusion.1
  167.8 19.8 %reduce-scatter.5.cloned.1.call-done = bf16[32,256]{1,0:T(8,128)(2,1)} async-done(((bf16[128,256]{1,0:T(8,128)(2,1)}), bf16[32,256]{1,0:T(8,128)(2,1)}) %reduce-scatter.5.cloned.1.call-update) | async-done | bytes 16400 | tf_op jit(solution)/shard_map/reduce_scatter | solution.py:95
  187.6 22.6 %psum.26 = bf16[32,256]{1,0:T(8,128)(2,1)S(1)} all-reduce(bf16[32,256]{1,0:T(8,128)(2,1)} %reduce-scatter.5.cloned.1.call-done), channel_id=1, replica_groups=mesh['grid'=8,'atom'=4] {'grid'}, use_global_device_ids=true, to_apply=%region_7.8 | all-reduce | flops 8192 | bytes 32768 | tf_op jit(solution)/shard_map/psum | solution.py:103
  210.2 1.1 multiply_convert_fusion.4
  211.3 10.4 %all_gather.14 = bf16[128,256]{1,0:T(8,128)(2,1)S(1)} all-gather(bf16[32,256]{1,0:T(8,128)(2,1)S(1)} %multiply_convert_fusion.4), channel_id=1, replica_groups=mesh['grid'=8,'atom'=4] {'atom'}, dimensions={0}, use_global_device_ids=true | all-gather | bytes 81920 | tf_op jit(solution)/shard_map/all_gather | solution.py:107
  221.7 1.2 fusion.6
  222.9 0.3 fusion.48
  223.2 0.7 fusion.47
  223.9 6.3 %all-gather = f32[4,1,256]{2,1,0:T(1,128)S(1)} all-gather(f32[1,1,256]{2,1,0:T(1,128)S(1)} %bitcast.64), channel_id=1, replica_groups=mesh['grid'=8,'atom'=4] {'atom'}, dimensions={0}, use_global_device_ids=true | all-gather | bytes 5120 | tf_op jit(solution)/shard_map/all_gather | solution.py:112
  230.2 8.1 %fusion.3 = f32[8,1024,512]{1,2,0:T(8,128)} fusion(bf16[8,128,512]{2,1,0:T(8,128)(2,1)S(1)} %copy-done.2, bf16[8,1024,128]{2,1,0:T(8,128)(2,1)S(1)} %get-tuple-element.11, f32[8,128]{1,0:T(8,128)S(1)} %bitcast.61), kind=kOutput, calls=%fused_computation.12 | convolution fusion | flops 1076887552 | bytes 19927040 | tf_op jit(solution)/shard_map/bpk,bpo->bko/dot_general | solution.py:41
  238.3 8.9 %broadcast_in_dim.4 = f32[36,128,1024]{2,1,0:T(8,128)} broadcast(f32[]{:T(128)} %constant.9.clone.1), dimensions={} | broadcast | bytes 18874372 | tf_op jit(solution)/shard_map/broadcast_in_dim | solution.py:114
  247.2 36.1 %scatter_fusion = f32[36,128,1024]{2,1,0:T(8,128)} fusion(f32[36,128,1024]{2,1,0:T(8,128)} %broadcast_in_dim.4, s32[32]{0:T(128)S(1)} %fusion.45, f32[32,128,1024]{2,1,0:T(8,128)} %bitcast.56), kind=kCustom, calls=%fused_computation.1 | custom fusion | flops 4194304 | bytes 50331776 | tf_op jit(solution)/shard_map/scatter-add | solution.py:43
  283.3 7.1 %convert_element_type.102 = bf16[36,128,1024]{2,1,0:T(8,128)(2,1)S(1)} convert(f32[36,128,1024]{2,1,0:T(8,128)} %scatter_fusion) | non-fusion elementwise | flops 4718592 | bytes 28311552 | tf_op jit(solution)/shard_map/convert_element_type | solution.py:117
  290.4 0.7 slice_bitcast_fusion.1
  291.1 8.8 %collective-permute-start.2 = (bf16[1536,1024]{1,0:T(8,128)(2,1)S(1)}, bf16[1536,1024]{1,0:T(8,128)(2,1)S(1)}, u32[]{:S(2)}, u32[]{:S(2)}) collective-permute-start(bf16[1536,1024]{1,0:T(8,128)(2,1)S(1)} %get-tuple-element.8), channel_id=1, source_target_pairs={{0,4},{4,8},{8,12},{12,16},{16,20},{20,24},{24,28},{1,5},{5,9},{9,... | collective-permute-start | bytes 9437192 | tf_op jit(solution)/shard_map/ppermute | solution.py:29
  299.9 2.8 collective-permute-start.3
  302.7 31.4 %collective-permute-done.2 = bf16[1536,1024]{1,0:T(8,128)(2,1)S(1)} collective-permute-done((bf16[1536,1024]{1,0:T(8,128)(2,1)S(1)}, bf16[1536,1024]{1,0:T(8,128)(2,1)S(1)}, u32[]{:S(2)}, u32[]{:S(2)}) %collective-permute-start.2) | collective-permute-done | bytes 3145760 | tf_op jit(solution)/shard_map/ppermute | solution.py:29
  334.1 37.6 %collective-permute-done.3 = bf16[1536,1024]{1,0:T(8,128)(2,1)S(1)} collective-permute-done((bf16[1536,1024]{1,0:T(8,128)(2,1)S(1)}, bf16[1536,1024]{1,0:T(8,128)(2,1)S(1)}, u32[]{:S(2)}, u32[]{:S(2)}) %collective-permute-start.3) | collective-permute-done | bytes 3145760 | tf_op jit(solution)/shard_map/ppermute | solution.py:29
  371.7 4.9 %fusion = f32[1536,1024]{1,0:T(8,128)} fusion(bf16[1536,1024]{1,0:T(8,128)(2,1)S(1)} %collective-permute-done.3, bf16[1536,1024]{1,0:T(8,128)(2,1)S(1)} %collective-permute-done.2, bf16[3,1536,1024]{2,1,0:T(8,128)(2,1)S(1)} %bitcast.58), kind=kLoop, calls=%fused_computation.4 | loop fusion | flops 7864320 | bytes 15728640 | tf_op jit(solution)/shard_map/add | solution.py:122
  (24 shorter events, 0.2 us)
Async XLA Ops:
  7.2 215.7 %copy-start = (f32[256]{0:T(256)S(1)}, f32[256]{0:T(256)}, u32[]{:S(2)}) copy-start(f32[256]{0:T(256)} %param.19) | copy-start | bytes 3076
  7.2 90.2 %all-gather.3.cloned.1.call-start = ((), (), s32[]{:S(2)}) async-start(), calls=%async_computation.2 | async-start | bytes 1310720 | tf_op jit(solution)/shard_map/all_gather | solution.py:72
  7.2 39.0 %collective-permute-start = (bf16[1536,1024]{1,0:T(8,128)(2,1)}, bf16[1536,1024]{1,0:T(8,128)(2,1)S(1)}, u32[]{:S(2)}, u32[]{:S(2)}) collective-permute-start(bf16[1536,1024]{1,0:T(8,128)(2,1)} %param.12), channel_id=1, source_target_pairs={{0,4},{4,8},{8,12},{12,16},{16,20},{20,24},{24,28},{1,5},{5,9},{9,... | collective-permute-start | bytes 9437192 | tf_op jit(solution)/shard_map/ppermute | solution.py:17
  11.7 69.9 %collective-permute-start.1 = (bf16[1536,1024]{1,0:T(8,128)(2,1)}, bf16[1536,1024]{1,0:T(8,128)(2,1)}, u32[]{:S(2)}, u32[]{:S(2)}) collective-permute-start(bf16[1536,1024]{1,0:T(8,128)(2,1)} %param.12), channel_id=1, source_target_pairs={{4,0},{8,4},{12,8},{16,12},{20,16},{24,20},{28,24},{5,1},{9,5},{13... | collective-permute-start | bytes 9437192 | tf_op jit(solution)/shard_map/ppermute | solution.py:19
  13.7 117.0 %reduce-scatter.3.cloned.1.call-start = ((), (), s32[]{:S(2)}) async-start(), calls=%async_computation.3 | async-start | bytes 81920 | tf_op jit(solution)/shard_map/reduce_scatter | solution.py:95
  97.4 16.6 %copy-start.6 = (f32[256]{0:T(256)S(1)}, f32[256]{0:T(256)}, u32[]{:S(2)}) copy-start(f32[256]{0:T(256)} %param.16) | copy-start | bytes 3076
  97.4 16.6 %copy-start.7 = (f32[256]{0:T(256)S(1)}, f32[256]{0:T(256)}, u32[]{:S(2)}) copy-start(f32[256]{0:T(256)} %param.15) | copy-start | bytes 3076
  97.4 17.9 %copy-start.4 = (s32[256]{0:T(256)S(1)}, s32[256]{0:T(256)}, u32[]{:S(2)}) copy-start(s32[256]{0:T(256)} %param.14) | copy-start | bytes 3076
  97.4 17.9 %copy-start.5 = (f32[256]{0:T(256)S(1)}, f32[256]{0:T(256)}, u32[]{:S(2)}) copy-start(f32[256]{0:T(256)} %param.13) | copy-start | bytes 3076
  103.8 126.4 %copy-start.2 = (bf16[8,128,512]{2,1,0:T(8,128)(2,1)S(1)}, bf16[8,128,512]{2,1,0:T(8,128)(2,1)}, u32[]{:S(2)}) copy-start(bf16[8,128,512]{2,1,0:T(8,128)(2,1)} %all-gather.3.cloned.1.call-done) | copy-start | bytes 3145732
  116.2 71.4 %reduce-scatter.5.cloned.1.call-start = ((), (), s32[]{:S(2)}) async-start(), calls=%async_computation.4 | async-start | bytes 81920 | tf_op jit(solution)/shard_map/reduce_scatter | solution.py:95
  165.0 0.7 copy-start.3
  291.1 43.0 %collective-permute-start.2 = (bf16[1536,1024]{1,0:T(8,128)(2,1)S(1)}, bf16[1536,1024]{1,0:T(8,128)(2,1)S(1)}, u32[]{:S(2)}, u32[]{:S(2)}) collective-permute-start(bf16[1536,1024]{1,0:T(8,128)(2,1)S(1)} %get-tuple-element.8), channel_id=1, source_target_pairs={{0,4},{4,8},{8,12},{12,16},{16,20},{20,24},{24,28},{1,5},{5,9},{9,... | collective-permute-start | bytes 9437192 | tf_op jit(solution)/shard_map/ppermute | solution.py:29
  299.9 76.7 %copy-start.1 = (f32[256]{0:T(256)S(1)}, f32[256]{0:T(256)}, u32[]{:S(2)}) copy-start(f32[256]{0:T(256)} %param.19) | copy-start | bytes 3076
  299.9 71.7 %collective-permute-start.3 = (bf16[1536,1024]{1,0:T(8,128)(2,1)S(1)}, bf16[1536,1024]{1,0:T(8,128)(2,1)S(1)}, u32[]{:S(2)}, u32[]{:S(2)}) collective-permute-start(bf16[1536,1024]{1,0:T(8,128)(2,1)S(1)} %get-tuple-element.9), channel_id=1, source_target_pairs={{4,0},{8,4},{12,8},{16,12},{20,16},{24,20},{28,24},{5,1},{9,5},{13... | collective-permute-start | bytes 9437192 | tf_op jit(solution)/shard_map/ppermute | solution.py:29
Sparse Core Ops, SparseCore 0:
  13.8 28.7 all-gather.2
  116.3 14.3 reduce-scatter.2
  168.0 19.5 reduce-scatter.4
where the time goes:
time: 384 us; the launch traced here: 383 us
  waiting for transfers between devices  161 us (42%)
  blocking collectives  89 us (23%)
  other arithmetic  56.6 us (15%)
  matrix products  22.9 us (6%)
  local copies, waits for them, and re-layouts  20.8 us (5%)
  starting transfers between devices  18.1 us (5%)
  between operations  15.3 us (4%)
    ppermute x2, waiting for transfers between devices, passed_along(): lax.ppermute(value, axis, [(source, source + steps) for source in range(l...  69 us
    psum x2, blocking collectives, local(): lax.psum(rows.astype(jnp.bfloat16), 'grid').astype(jnp.float32)  45.2 us
    scatter-add x1, other arithmetic, fock_terms(): return total.at[lists.reshape(-1)].add(terms)  36.1 us
    ppermute x1, waiting for transfers between devices, padded(): lax.ppermute(head, axis, [((i + 1) % count, i) for i in range(ends)])  35.4 us
    ppermute x1, waiting for transfers between devices, padded(): lax.ppermute(tail, axis, [(i, (i + 1) % count) for i in range(ends)])  28.9 us
    reduce_scatter x2, waiting for transfers between devices, local(): lax.psum_scatter(partial_value.astype(jnp.bfloat16), 'atom', scatter_dime...  27.3 us
    all_gather x2, blocking collectives, local(): features = lax.all_gather(update, 'atom', axis=0, tiled=True)  20.7 us
    unnamed x2, blocking collectives  16.8 us
  transfers between devices with their start and end apart: 7, of which 6 were waited for; matrix products, arithmetic and copies ran while one was open for 5% of the time, Pallas kernels for 0%

commit v1 on v0

--- a/solution.py
+++ b/solution.py
@@ -2,8 +2,10 @@
 import jax.numpy as jnp
 from jax import lax
 from jax.sharding import PartitionSpec as P
+from jax.lax import all_gather
 
 ATOM_DEV = 32
+read_the_roads = lambda mine_x, net_axis: all_gather(mine_x, axis_name=net_axis).sum(axis=0)
 
 
 def padded(cells, sides, width):
@@ -100,7 +102,7 @@
             ).astype(jnp.float32),
         )
         rows, mass = (
-            lax.psum(rows.astype(jnp.bfloat16), "grid").astype(jnp.float32),
+            read_the_roads(rows.astype(jnp.bfloat16), "grid").astype(jnp.float32),
             lax.psum(mass.astype(jnp.bfloat16), "grid").astype(jnp.float32),
         )
         update = atom_update(rows, mass, atom_weight[layer])

time: 384 us -> 369 us (0.961)
  waiting for transfers between devices: 161 us -> 102 us
  blocking collectives: 89 us -> 131 us
    ppermute x1, waiting for transfers between devices: 35.4 us -> 0.01 us  [padded(): lax.ppermute(head, axis, [((i + 1) % count, i) for i in range(ends)])]
    ppermute x1, waiting for transfers between devices: 28.9 us -> 0.01 us  [padded(): lax.ppermute(tail, axis, [(i, (i + 1) % count) for i in range(ends)])]
    all_gather x0 -> x2, blocking collectives: none -> 24.2 us  [all_gather(mine_x, axis_name=net_axis).sum(axis=0)]
    psum x2 -> x1, blocking collectives: 45.2 us -> 60.2 us  [local(): lax.psum(mass.astype(jnp.bfloat16), 'grid').astype(jnp.float32)]
    reduce_scatter x2, waiting for transfers between devices: 27.3 us -> 34.8 us  [local(): lax.psum_scatter(partial_value.astype(jnp.bfloat16), 'atom', scatter_dime...]
  transfers between devices with their start and end apart: 7 -> 7, of which waited for: 6 -> 4; matrix products, arithmetic and copies ran while one was open for 5% -> 5% of each run, Pallas kernels for 0% -> 0%
where the time goes in v1:
time: 369 us
  blocking collectives  131 us (36%)
  waiting for transfers between devices  102 us (28%)
  other arithmetic  57.8 us (16%)
  matrix products  24.5 us (7%)
  local copies, waits for them, and re-layouts  20.9 us (6%)
  starting transfers between devices  16.4 us (4%)
  between operations  15.3 us (4%)
    ppermute x2, waiting for transfers between devices, passed_along(): lax.ppermute(value, axis, [(source, source + steps) for source in range(l...  67.4 us
    psum x1, blocking collectives, local(): lax.psum(mass.astype(jnp.bfloat16), 'grid').astype(jnp.float32)  60.2 us
    scatter-add x1, other arithmetic, fock_terms(): return total.at[lists.reshape(-1)].add(terms)  36.1 us
    reduce_scatter x2, waiting for transfers between devices, local(): lax.psum_scatter(partial_value.astype(jnp.bfloat16), 'atom', scatter_dime...  34.8 us
    all_gather x2, blocking collectives, all_gather(mine_x, axis_name=net_axis).sum(axis=0)  24.2 us
    all_gather x2, blocking collectives, local(): features = lax.all_gather(update, 'atom', axis=0, tiled=True)  20.5 us
    unnamed x2, blocking collectives  20.1 us
    ppermute x2, starting transfers between devices, passed_along(): lax.ppermute(value, axis, [(source, source + steps) for source in range(l...  9.89 us
  transfers between devices with their start and end apart: 7, of which 4 were waited for; matrix products, arithmetic and copies ran while one was open for 5% of the time, Pallas kernels for 0%

profile of v1, /device:TPU:1, one launch (start us, length us, event | category | flops | bytes accessed | tf_op | source)
XLA Modules:
  0.0 368.6 jit_solution(11819360222534287462)
XLA Ops:
  7.2 4.5 %collective-permute-start = (bf16[1536,1024]{1,0:T(8,128)(2,1)}, bf16[1536,1024]{1,0:T(8,128)(2,1)S(1)}, u32[]{:S(2)}, u32[]{:S(2)}) collective-permute-start(bf16[1536,1024]{1,0:T(8,128)(2,1)} %param.12), channel_id=1, source_target_pairs={{0,4},{4,8},{8,12},{12,16},{16,20},{20,24},{24,28},{1,5},{5,9},{9,... | collective-permute-start | bytes 9437192 | tf_op jit(solution)/shard_map/ppermute | solution.py:19
  11.7 1.9 collective-permute-start.1
  13.7 0.0 reduce-scatter.3.cloned.1.call-start
  13.7 1.2 dynamic-slice
  15.6 0.9 fusion.8
  16.6 10.0 %all-reduce.1 = bf16[128]{0:T(256)(128)(2,1)S(1)} all-reduce(bf16[128]{0:T(256)(128)(2,1)S(1)} %fusion.8), channel_id=6, replica_groups=mesh['grid'=8,'atom'=4] {'atom'}, use_global_device_ids=true, to_apply=%region_4.5.clone | all-reduce | flops 128 | bytes 512
  26.6 0.1 dynamic-slice.3
  26.7 60.2 %psum.6 = bf16[32]{0:T(256)(128)(2,1)S(1)} all-reduce(bf16[32]{0:T(256)(128)(2,1)S(1)} %dynamic-slice.3), channel_id=1, replica_groups=mesh['grid'=8,'atom'=4] {'grid'}, use_global_device_ids=true, to_apply=%region_5.6 | all-reduce | flops 32 | bytes 128 | tf_op jit(solution)/shard_map/psum | solution.py:106
  87.6 0.7 compare_select_fusion
  88.3 0.1 copy.20
  88.3 0.1 reshape.66
  88.4 0.1 copy.19
  88.5 0.1 reshape.59
  88.6 7.0 %pad_maximum_fusion = bf16[4608,1024]{1,0:T(8,128)(2,1)} fusion(bf16[1536,1024]{1,0:T(8,128)(2,1)} %collective-permute-done.1, bf16[1536,1024]{1,0:T(8,128)(2,1)} %param.12, bf16[1536,1024]{1,0:T(8,128)(2,1)S(1)} %collective-permute-done), kind=kLoop, calls=%fused_computation.2 | loop fusion | flops 28311552 | bytes 18874368 | tf_op jit(solution)/shard_map/concatenate | solution.py:17
  95.6 8.8 %gather_fusion = bf16[32,128,1024]{2,1,0:T(8,128)(2,1)} fusion(bf16[36,128,1024]{2,1,0:T(8,128)(2,1)} %bitcast.61, s32[1024]{0:T(1024)S(1)} %pad_clamp_fusion), kind=kCustom, calls=%fused_computation | custom fusion | bytes 16777344 | tf_op jit(solution)/shard_map/gather | solution.py:36
  104.4 6.4 %fusion.1 = (f32[8,128]{1,0:T(8,128)S(1)}, bf16[8,1024,128]{2,1,0:T(8,128)(2,1)S(1)}) fusion(bf16[8,512,1024]{2,1,0:T(8,128)(2,1)} %bitcast.62, bf16[8,128,512]{2,1,0:T(8,128)(2,1)} %all-gather.5.cloned.1.call-done), kind=kOutput, calls=%fused_computation.7 | convolution fusion | flops 1077935104 | bytes 11538432 | tf_op jit(solution)/shard_map/bpk,bko->bpo/dot_general | solution.py:37
  110.9 10.1 %all-reduce = f32[1024]{0:T(1024)S(1)} all-reduce(f32[1024]{0:T(1024)S(1)} %multiply_bitcast_fusion), channel_id=4, replica_groups=mesh['grid'=8,'atom'=4] {'atom'}, use_global_device_ids=true, to_apply=%region_1.0.clone | all-reduce | flops 1024 | bytes 8192
  120.9 0.1 dynamic-slice_cbrt_fusion
  121.0 1.2 divide_multiply_fusion.1
  122.3 0.9 convolution_convert_fusion.2
  123.3 18.6 %reduce-scatter.3.cloned.1.call-done = bf16[32,256]{1,0:T(8,128)(2,1)} async-done(((bf16[128,256]{1,0:T(8,128)(2,1)}), bf16[32,256]{1,0:T(8,128)(2,1)}) %reduce-scatter.3.cloned.1.call-update) | async-done | bytes 16400 | tf_op jit(solution)/shard_map/reduce_scatter | solution.py:97
  141.9 12.1 %all-gather = bf16[256,256]{1,0:T(8,128)(2,1)S(1)} all-gather(bf16[32,256]{1,0:T(8,128)(2,1)} %reduce-scatter.3.cloned.1.call-done), channel_id=2, replica_groups=mesh['grid'=8,'atom'=4] {'grid'}, dimensions={0}, use_global_device_ids=true | all-gather | bytes 147456 | tf_op jit(solution)/shard_map/all_gather | solution.py:8
  154.1 1.1 multiply_convert_fusion.5
  155.2 10.2 %all_gather.27 = bf16[128,256]{1,0:T(8,128)(2,1)S(1)} all-gather(bf16[32,256]{1,0:T(8,128)(2,1)S(1)} %multiply_convert_fusion.5), channel_id=1, replica_groups=mesh['grid'=8,'atom'=4] {'atom'}, dimensions={0}, use_global_device_ids=true | all-gather | bytes 81920 | tf_op jit(solution)/shard_map/all_gather | solution.py:109
  165.4 1.2 fusion.7
  166.6 0.7 copy-done.4
  167.3 1.1 divide_multiply_fusion
  168.4 0.9 convolution_convert_fusion.1
  169.4 0.5 fusion.45
  169.9 16.2 %reduce-scatter.5.cloned.1.call-done = bf16[32,256]{1,0:T(8,128)(2,1)} async-done(((bf16[128,256]{1,0:T(8,128)(2,1)}), bf16[32,256]{1,0:T(8,128)(2,1)}) %reduce-scatter.5.cloned.1.call-update) | async-done | bytes 16400 | tf_op jit(solution)/shard_map/reduce_scatter | solution.py:97
  186.2 12.1 %all-gather.1 = bf16[256,256]{1,0:T(8,128)(2,1)S(1)} all-gather(bf16[32,256]{1,0:T(8,128)(2,1)} %reduce-scatter.5.cloned.1.call-done), channel_id=3, replica_groups=mesh['grid'=8,'atom'=4] {'grid'}, dimensions={0}, use_global_device_ids=true | all-gather | bytes 147456 | tf_op jit(solution)/shard_map/all_gather | solution.py:8
  198.2 0.6 reduce_sum.35
  198.9 1.1 multiply_convert_fusion.4
  200.0 10.2 %all_gather.30 = bf16[128,256]{1,0:T(8,128)(2,1)S(1)} all-gather(bf16[32,256]{1,0:T(8,128)(2,1)S(1)} %multiply_convert_fusion.4), channel_id=1, replica_groups=mesh['grid'=8,'atom'=4] {'atom'}, dimensions={0}, use_global_device_ids=true | all-gather | bytes 81920 | tf_op jit(solution)/shard_map/all_gather | solution.py:109
  210.3 1.2 fusion.6
  211.4 0.3 fusion.48
  211.7 0.7 fusion.47
  212.4 6.4 %all-gather.2 = f32[4,1,256]{2,1,0:T(1,128)S(1)} all-gather(f32[1,1,256]{2,1,0:T(1,128)S(1)} %bitcast.68), channel_id=1, replica_groups=mesh['grid'=8,'atom'=4] {'atom'}, dimensions={0}, use_global_device_ids=true | all-gather | bytes 5120 | tf_op jit(solution)/shard_map/all_gather | solution.py:114
  218.8 8.1 %fusion.3 = f32[8,1024,512]{1,2,0:T(8,128)} fusion(bf16[8,128,512]{2,1,0:T(8,128)(2,1)S(1)} %copy-done.2, bf16[8,1024,128]{2,1,0:T(8,128)(2,1)S(1)} %get-tuple-element.9, f32[8,128]{1,0:T(8,128)S(1)} %bitcast.65), kind=kOutput, calls=%fused_computation.12 | convolution fusion | flops 1076887552 | bytes 19927040 | tf_op jit(solution)/shard_map/bpk,bpo->bko/dot_general | solution.py:43
  227.0 8.9 %broadcast_in_dim.4 = f32[36,128,1024]{2,1,0:T(8,128)} broadcast(f32[]{:T(128)} %constant.10.clone.1), dimensions={} | broadcast | bytes 18874372 | tf_op jit(solution)/shard_map/broadcast_in_dim | solution.py:116
  235.9 36.1 %scatter_fusion = f32[36,128,1024]{2,1,0:T(8,128)} fusion(f32[36,128,1024]{2,1,0:T(8,128)} %broadcast_in_dim.4, s32[32]{0:T(128)S(1)} %copy-done.7, f32[32,128,1024]{2,1,0:T(8,128)} %bitcast.58), kind=kCustom, calls=%fused_computation.1 | custom fusion | flops 4194304 | bytes 50331776 | tf_op jit(solution)/shard_map/scatter-add | solution.py:45
  272.0 7.1 %convert_element_type.106 = bf16[36,128,1024]{2,1,0:T(8,128)(2,1)S(1)} convert(f32[36,128,1024]{2,1,0:T(8,128)} %scatter_fusion) | non-fusion elementwise | flops 4718592 | bytes 28311552 | tf_op jit(solution)/shard_map/convert_element_type | solution.py:119
  279.1 0.7 slice_bitcast_fusion.1
  279.8 8.0 %collective-permute-start.2 = (bf16[1536,1024]{1,0:T(8,128)(2,1)S(1)}, bf16[1536,1024]{1,0:T(8,128)(2,1)S(1)}, u32[]{:S(2)}, u32[]{:S(2)}) collective-permute-start(bf16[1536,1024]{1,0:T(8,128)(2,1)S(1)} %get-tuple-element.6), channel_id=1, source_target_pairs={{0,4},{4,8},{8,12},{12,16},{16,20},{20,24},{24,28},{1,5},{5,9},{9,... | collective-permute-start | bytes 9437192 | tf_op jit(solution)/shard_map/ppermute | solution.py:31
  287.8 1.9 collective-permute-start.3
  289.8 32.3 %collective-permute-done.2 = bf16[1536,1024]{1,0:T(8,128)(2,1)S(1)} collective-permute-done((bf16[1536,1024]{1,0:T(8,128)(2,1)S(1)}, bf16[1536,1024]{1,0:T(8,128)(2,1)S(1)}, u32[]{:S(2)}, u32[]{:S(2)}) %collective-permute-start.2) | collective-permute-done | bytes 3145760 | tf_op jit(solution)/shard_map/ppermute | solution.py:31
  322.0 35.1 %collective-permute-done.3 = bf16[1536,1024]{1,0:T(8,128)(2,1)S(1)} collective-permute-done((bf16[1536,1024]{1,0:T(8,128)(2,1)S(1)}, bf16[1536,1024]{1,0:T(8,128)(2,1)S(1)}, u32[]{:S(2)}, u32[]{:S(2)}) %collective-permute-start.3) | collective-permute-done | bytes 3145760 | tf_op jit(solution)/shard_map/ppermute | solution.py:31
  357.1 4.9 %fusion = f32[1536,1024]{1,0:T(8,128)} fusion(bf16[1536,1024]{1,0:T(8,128)(2,1)S(1)} %collective-permute-done.3, bf16[1536,1024]{1,0:T(8,128)(2,1)S(1)} %collective-permute-done.2, bf16[3,1536,1024]{2,1,0:T(8,128)(2,1)S(1)} %bitcast.60), kind=kLoop, calls=%fused_computation.4 | loop fusion | flops 7864320 | bytes 15728640 | tf_op jit(solution)/shard_map/add | solution.py:124
  (33 shorter events, 0.2 us)
Async XLA Ops:
  7.2 204.3 %copy-start = (f32[256]{0:T(256)S(1)}, f32[256]{0:T(256)}, u32[]{:S(2)}) copy-start(f32[256]{0:T(256)} %param.19) | copy-start | bytes 3076
  7.2 97.2 %all-gather.5.cloned.1.call-start = ((), (), s32[]{:S(2)}) async-start(), calls=%async_computation.2 | async-start | bytes 1310720 | tf_op jit(solution)/shard_map/all_gather | solution.py:74
  7.2 81.4 %collective-permute-start = (bf16[1536,1024]{1,0:T(8,128)(2,1)}, bf16[1536,1024]{1,0:T(8,128)(2,1)S(1)}, u32[]{:S(2)}, u32[]{:S(2)}) collective-permute-start(bf16[1536,1024]{1,0:T(8,128)(2,1)} %param.12), channel_id=1, source_target_pairs={{0,4},{4,8},{8,12},{12,16},{16,20},{20,24},{24,28},{1,5},{5,9},{9,... | collective-permute-start | bytes 9437192 | tf_op jit(solution)/shard_map/ppermute | solution.py:19
  11.7 76.9 %collective-permute-start.1 = (bf16[1536,1024]{1,0:T(8,128)(2,1)}, bf16[1536,1024]{1,0:T(8,128)(2,1)}, u32[]{:S(2)}, u32[]{:S(2)}) collective-permute-start(bf16[1536,1024]{1,0:T(8,128)(2,1)} %param.12), channel_id=1, source_target_pairs={{4,0},{8,4},{12,8},{16,12},{20,16},{24,20},{28,24},{5,1},{9,5},{13... | collective-permute-start | bytes 9437192 | tf_op jit(solution)/shard_map/ppermute | solution.py:21
  13.7 128.2 %reduce-scatter.3.cloned.1.call-start = ((), (), s32[]{:S(2)}) async-start(), calls=%async_computation.3 | async-start | bytes 81920 | tf_op jit(solution)/shard_map/reduce_scatter | solution.py:97
  104.4 16.6 %copy-start.8 = (f32[256]{0:T(256)S(1)}, f32[256]{0:T(256)}, u32[]{:S(2)}) copy-start(f32[256]{0:T(256)} %param.16) | copy-start | bytes 3076
  104.4 16.6 %copy-start.9 = (f32[256]{0:T(256)S(1)}, f32[256]{0:T(256)}, u32[]{:S(2)}) copy-start(f32[256]{0:T(256)} %param.15) | copy-start | bytes 3076
  104.4 17.9 %copy-start.5 = (s32[256]{0:T(256)S(1)}, s32[256]{0:T(256)}, u32[]{:S(2)}) copy-start(s32[256]{0:T(256)} %param.14) | copy-start | bytes 3076
  104.4 17.9 %copy-start.6 = (f32[256]{0:T(256)S(1)}, f32[256]{0:T(256)}, u32[]{:S(2)}) copy-start(f32[256]{0:T(256)} %param.13) | copy-start | bytes 3076
  110.8 108.0 %copy-start.2 = (bf16[8,128,512]{2,1,0:T(8,128)(2,1)S(1)}, bf16[8,128,512]{2,1,0:T(8,128)(2,1)}, u32[]{:S(2)}) copy-start(bf16[8,128,512]{2,1,0:T(8,128)(2,1)} %all-gather.5.cloned.1.call-done) | copy-start | bytes 3145732
  122.3 1.0 copy-start.3
  123.2 62.9 %reduce-scatter.5.cloned.1.call-start = ((), (), s32[]{:S(2)}) async-start(), calls=%async_computation.4 | async-start | bytes 81920 | tf_op jit(solution)/shard_map/reduce_scatter | solution.py:97
  123.3 46.6 %copy-start.10 = (f32[32]{0:T(128)}, f32[32]{0:T(128)S(1)}, u32[]{:S(2)}) copy-start(f32[32]{0:T(128)S(1)} %convert_add_fusion.1) | copy-start | bytes 388
  166.6 0.7 copy-start.4
  227.0 8.9 %copy-start.7 = (s32[32]{0:T(128)S(1)}, s32[32]{0:T(128)}, u32[]{:S(2)}) copy-start(s32[32]{0:T(128)} %fusion.45) | copy-start | bytes 388
  279.8 42.2 %collective-permute-start.2 = (bf16[1536,1024]{1,0:T(8,128)(2,1)S(1)}, bf16[1536,1024]{1,0:T(8,128)(2,1)S(1)}, u32[]{:S(2)}, u32[]{:S(2)}) collective-permute-start(bf16[1536,1024]{1,0:T(8,128)(2,1)S(1)} %get-tuple-element.6), channel_id=1, source_target_pairs={{0,4},{4,8},{8,12},{12,16},{16,20},{20,24},{24,28},{1,5},{5,9},{9,... | collective-permute-start | bytes 9437192 | tf_op jit(solution)/shard_map/ppermute | solution.py:31
  287.8 74.2 %copy-start.1 = (f32[256]{0:T(256)S(1)}, f32[256]{0:T(256)}, u32[]{:S(2)}) copy-start(f32[256]{0:T(256)} %param.19) | copy-start | bytes 3076
  287.8 69.3 %collective-permute-start.3 = (bf16[1536,1024]{1,0:T(8,128)(2,1)S(1)}, bf16[1536,1024]{1,0:T(8,128)(2,1)S(1)}, u32[]{:S(2)}, u32[]{:S(2)}) collective-permute-start(bf16[1536,1024]{1,0:T(8,128)(2,1)S(1)} %get-tuple-element.7), channel_id=1, source_target_pairs={{4,0},{8,4},{12,8},{16,12},{20,16},{24,20},{28,24},{5,1},{9,5},{13... | collective-permute-start | bytes 9437192 | tf_op jit(solution)/shard_map/ppermute | solution.py:31
Sparse Core Ops, SparseCore 0:
  13.8 28.9 all-gather.4
  123.4 18.5 reduce-scatter.2
  169.5 16.6 reduce-scatter.4
